TPU v7x, 32 devices: a whole 2x2x4 slice. The times are simulated.
32 devices in a mesh: dp: 4 (over x, core), mp: 8 (over z, y).
Axes of the slice: x: 2, y: 2, z: 4, core: 2. Of those that a mesh axis runs over, the one named last changes fastest.
Arguments:
- tokens: bfloat16 [1280, 1792], P(('dp', 'mp')), may hold values from -6 to 6
- norm_gain: float32 [1792], replicated, may hold values from 0.5 to 1.5
- norm_bias: float32 [1792], replicated, may hold values from -3 to 3
- w_in: bfloat16 [1792, 15360], P('dp', 'mp'), may hold values from -0.125 to 0.125
- b_in: float32 [15360], P('mp'), may hold values from -3 to 3
- w_out: bfloat16 [15360, 1792], P('mp', 'dp'), may hold values from -0.046875 to 0.046875
- b_out: float32 [1792], replicated, may hold values from -3 to 3
Outputs:
- result: bfloat16 [1280, 1792], P(('dp', 'mp'))
All inputs are finite; a program needn't handle non-finite values.
Results may differ from a plain program's by a relative error of at most 0.0042.
Values may be sent and summed in bfloat16 or wider, within the bound.
A program may use at most 128 MiB of HBM per device.

v0:
```python
import jax
import jax.numpy as jnp
from jax import lax
from jax.sharding import PartitionSpec as P


def on_device(tokens, norm_gain, norm_bias, w_in, b_in, w_out, b_out):
    values = tokens.astype(jnp.float32)
    center = jnp.mean(values, axis=1, keepdims=True)
    spread = jnp.mean((values - center) ** 2, axis=1, keepdims=True)
    normed = ((values - center) / jnp.sqrt(spread + 1e-06) * norm_gain + norm_bias).astype(
        jnp.bfloat16
    )
    w_in_full = lax.all_gather(w_in, "dp", axis=0, tiled=True)
    gathered = lax.all_gather(normed, "mp", axis=0, tiled=True)
    pre = jnp.dot(gathered, w_in_full, preferred_element_type=jnp.float32) + b_in
    hidden = jax.nn.gelu(pre, approximate=False).astype(jnp.bfloat16)
    w_out_full = lax.all_gather(w_out, "dp", axis=1, tiled=True)
    summed = lax.psum_scatter(
        jnp.dot(hidden, w_out_full, preferred_element_type=jnp.float32),
        "mp",
        scatter_dimension=0,
        tiled=True,
    )
    return (values + summed + b_out).astype(jnp.bfloat16)


def solution(mesh):
    placed = (P(("dp", "mp"), None), P(), P(), P("dp", "mp"), P("mp"), P("mp", "dp"), P())
    return jax.shard_map(
        on_device, mesh=mesh, in_specs=placed, out_specs=P(("dp", "mp"), None), check_vma=False
    )
```

profile of v0, /device:TPU:0, one launch (start us, length us, event | category | flops | bytes accessed | tf_op | source)
XLA Modules:
  0.0 249.3 jit_solution(16586171305829466705)
XLA Ops:
  6.5 0.0 copy-start.2
  6.5 0.0 all-gather.4.cloned.1.call-start
  6.5 1.0 convert_reduce_fusion
  7.6 1.1 fusion.45
  8.7 1.7 fusion.48
  10.5 0.0 all-gather.4.cloned.1.call-update
  10.5 0.0 all-gather.6.cloned.1.call-start
  10.5 0.7 all-gather.6.cloned.1.call-update
  11.2 0.0 all-gather.8.cloned.1.call-start
  11.3 0.7 all-gather.8.cloned.1.call-update
  12.0 0.0 copy-start
  12.0 0.0 copy-start.1
  12.0 0.0 reduce-scatter.2.cloned.1.call-start
  12.0 42.5 %all-gather.4.cloned.1.call-done = bf16[320,1792]{1,0:T(8,128)(2,1)} async-done(((bf16[40,1792]{1,0:T(8,128)(2,1)}), bf16[320,1792]{1,0:T(8,128)(2,1)}) %all-gather.4.cloned.1.call-update) | async-done | bytes 1146896 | tf_op jit(solution)/shard_map/all_gather | solution.py:15
  54.6 49.7 %all-gather.6.cloned.1.call-done = bf16[1792,1920]{1,0:T(8,128)(2,1)} async-done(((bf16[448,1920]{1,0:T(8,128)(2,1)}), bf16[1792,1920]{1,0:T(8,128)(2,1)}) %all-gather.6.cloned.1.call-update) | async-done | bytes 6881296 | tf_op jit(solution)/shard_map/all_gather | solution.py:14
  104.3 51.3 %all-gather.8.cloned.1.call-done = bf16[1920,1792]{0,1:T(8,128)(2,1)} async-done(((bf16[1920,448]{0,1:T(8,128)(2,1)}), bf16[1920,1792]{0,1:T(8,128)(2,1)}) %all-gather.8.cloned.1.call-update) | async-done | bytes 6881296 | tf_op jit(solution)/shard_map/all_gather | solution.py:18
  155.6 0.0 copy-done.2
  155.6 15.7 %fusion.10 = f32[320,1792]{1,0:T(8,128)} fusion(bf16[1920,1792]{0,1:T(8,128)(2,1)} %all-gather.8.cloned.1.call-done, bf16[320,1792]{1,0:T(8,128)(2,1)} %all-gather.4.cloned.1.call-done, bf16[1792,1920]{1,0:T(8,128)(2,1)} %all-gather.6.cloned.1.call-done, f32[1920]{0:T(1024)S(1)} %copy-done.2), kind=kOutput, calls=%fused_computation.20 | convolution fusion | flops 4444569600 | bytes 17210880 | tf_op jit(solution)/shard_map/dot_general | solution.py:20
  171.3 0.0 reduce-scatter.2.cloned.1.call-update
  171.4 69.7 %reduce-scatter.2.cloned.1.call-done = f32[40,1792]{1,0:T(8,128)} async-done(((f32[320,1792]{1,0:T(8,128)}), f32[40,1792]{1,0:T(8,128)}) %reduce-scatter.2.cloned.1.call-update) | async-done | bytes 286736 | tf_op jit(solution)/shard_map/reduce_scatter | solution.py:19
  241.1 0.0 copy-done
  241.1 0.0 copy-done.1
  241.1 1.7 fusion.50
  (2 shorter events, 0.0 us)
Async XLA Ops:
  6.5 149.1 %copy-start.2 = (f32[1920]{0:T(1024)S(1)}, f32[1920]{0:T(1024)}, u32[]{:S(2)}) copy-start(f32[1920]{0:T(1024)} %param.11) | copy-start | bytes 23044
  6.5 48.0 %all-gather.4.cloned.1.call-start = ((), (), s32[]{:S(2)}) async-start(), calls=%async_computation.1 | async-start | bytes 1290240 | tf_op jit(solution)/shard_map/all_gather | solution.py:15
  10.5 93.8 %all-gather.6.cloned.1.call-start = ((), (), s32[]{:S(2)}) async-start(), calls=%async_computation.2 | async-start | bytes 8601600 | tf_op jit(solution)/shard_map/all_gather | solution.py:14
  11.2 144.4 %all-gather.8.cloned.1.call-start = ((), (), s32[]{:S(2)}) async-start(), calls=%async_computation.3 | async-start | bytes 8601600 | tf_op jit(solution)/shard_map/all_gather | solution.py:18
  12.0 229.1 %copy-start = (bf16[40,1792]{1,0:T(8,128)(2,1)S(1)}, bf16[40,1792]{1,0:T(8,128)(2,1)}, u32[]{:S(2)}) copy-start(bf16[40,1792]{1,0:T(8,128)(2,1)} %param.7) | copy-start | bytes 430084
  12.0 229.1 %copy-start.1 = (f32[1792]{0:T(1024)S(1)}, f32[1792]{0:T(1024)}, u32[]{:S(2)}) copy-start(f32[1792]{0:T(1024)} %param.13) | copy-start | bytes 21508
  12.0 229.1 %reduce-scatter.2.cloned.1.call-start = ((), (), s32[]{:S(2)}) async-start(), calls=%async_computation.4 | async-start | bytes 2580480 | tf_op jit(solution)/shard_map/reduce_scatter | solution.py:19
Sparse Core Ops, SparseCore 0:
  10.6 43.9 all-gather.3
  56.1 48.1 all-gather.5
  105.9 49.6 all-gather.7
  171.5 69.5 reduce-scatter.1
where the time goes:
time: 249 us
  waiting for transfers between devices  215 us (86%)
  matrix products  15.7 us (6%)
  between operations  13.2 us (5%)
  other arithmetic  5.56 us (2%)
    reduce_scatter x1, waiting for transfers between devices, on_device(): lax.psum_scatter(jnp.dot(hidden, w_out_full, preferred_element_type=jnp.f...  69.7 us
    all_gather x1, waiting for transfers between devices, on_device(): w_out_full = lax.all_gather(w_out, 'dp', axis=1, tiled=True)  51.3 us
    all_gather x1, waiting for transfers between devices, on_device(): w_in_full = lax.all_gather(w_in, 'dp', axis=0, tiled=True)  49.7 us
    all_gather x1, waiting for transfers between devices, on_device(): gathered = lax.all_gather(normed, 'mp', axis=0, tiled=True)  42.5 us
    dot_general x1, matrix products, on_device(): jnp.dot(hidden, w_out_full, preferred_element_type=jnp.float32)  15.7 us
  transfers between devices with their start and end apart: 4, of which 4 were waited for; matrix products, arithmetic and copies ran while one was open for 0% of the time, Pallas kernels for 0%

commit v1 on v0

--- a/solution.py
+++ b/solution.py
@@ -2,6 +2,7 @@
 import jax.numpy as jnp
 from jax import lax
 from jax.sharding import PartitionSpec as P
+from jax.lax import axis_index, ppermute, psum
 
 
 def on_device(tokens, norm_gain, norm_bias, w_in, b_in, w_out, b_out):
@@ -15,7 +16,20 @@
     gathered = lax.all_gather(normed, "mp", axis=0, tiled=True)
     pre = jnp.dot(gathered, w_in_full, preferred_element_type=jnp.float32) + b_in
     hidden = jax.nn.gelu(pre, approximate=False).astype(jnp.bfloat16)
-    w_out_full = lax.all_gather(w_out, "dp", axis=1, tiled=True)
+
+    def press_sample(content, pos_dim):
+        dev_count = psum(1, axis_name="dp")
+        items = [content]
+        for num in tuple(range(dev_count - 1)):
+            found_now = ppermute(
+                items[-1], axis_name="dp", perm=[(b, (b + 1) % dev_count) for b in range(dev_count)]
+            )
+            items.append(found_now)
+        val = jnp.concatenate(items[::-1], axis=pos_dim)
+        e_next = axis_index("dp")
+        return jnp.roll(val, shift=(e_next + 1) * content.shape[pos_dim], axis=pos_dim)
+
+    w_out_full = press_sample(w_out, pos_dim=1)
     summed = lax.psum_scatter(
         jnp.dot(hidden, w_out_full, preferred_element_type=jnp.float32),
         "mp",

time: 249 us -> 216 us (0.87)
  waiting for transfers between devices: 215 us -> 164 us
  local copies, waits for them, and re-layouts: 0.02 us -> 16.7 us
    ppermute x0 -> x3, waiting for transfers between devices: none -> 86.9 us  [press_sample(): ppermute(items[-1], axis_name='dp', perm=[(b, (b + 1) % dev_count) for b...]
    all_gather x1 -> x0, waiting for transfers between devices: 51.3 us -> none  [on_device(): w_out_full = lax.all_gather(w_out, 'dp', axis=1, tiled=True)]
    all_gather x1, waiting for transfers between devices: 49.7 us -> 0.01 us  [on_device(): w_in_full = lax.all_gather(w_in, 'dp', axis=0, tiled=True)]
    all_gather x1, waiting for transfers between devices: 42.5 us -> 0.01 us  [on_device(): gathered = lax.all_gather(normed, 'mp', axis=0, tiled=True)]
    unnamed x6 -> x15, local copies, waits for them, and re-layouts: 0.02 us -> 15.3 us
    reduce_scatter x1, waiting for transfers between devices: 69.7 us -> 75.9 us  [on_device(): lax.psum_scatter(jnp.dot(hidden, w_out_full, preferred_element_type=jnp.f...]
  transfers between devices with their start and end apart: 4 -> 6, of which waited for: 4 -> 4; matrix products, arithmetic and copies ran while one was open for 0% -> 8% of each run, Pallas kernels for 0% -> 0%
where the time goes in v1:
time: 216 us
  waiting for transfers between devices  164 us (76%)
  local copies, waits for them, and re-layouts  16.7 us (8%)
  matrix products  16 us (7%)
  between operations  13.1 us (6%)
  other arithmetic  5.68 us (3%)
    ppermute x3, waiting for transfers between devices, press_sample(): ppermute(items[-1], axis_name='dp', perm=[(b, (b + 1) % dev_count) for b...  86.9 us
    reduce_scatter x1, waiting for transfers between devices, on_device(): lax.psum_scatter(jnp.dot(hidden, w_out_full, preferred_element_type=jnp.f...  75.9 us
    dot_general x1, matrix products, on_device(): jnp.dot(hidden, w_out_full, preferred_element_type=jnp.float32)  16 us
    unnamed x15, local copies, waits for them, and re-layouts  15.3 us
  transfers between devices with their start and end apart: 6, of which 4 were waited for; matrix products, arithmetic and copies ran while one was open for 8% of the time, Pallas kernels for 0%

profile of v1, /device:TPU:0, one launch (start us, length us, event | category | flops | bytes accessed | tf_op | source)
XLA Modules:
  0.0 215.7 jit_solution(12784724411709924408)
XLA Ops:
  6.5 0.0 copy-start
  6.5 0.0 all-gather.3.cloned.1.call-start
  6.5 1.2 convert_reduce_fusion
  7.7 1.1 fusion.46
  8.8 1.7 fusion.49
  10.6 0.0 all-gather.3.cloned.1.call-update
  10.6 0.0 all-gather.5.cloned.1.call-start
  10.6 0.7 all-gather.5.cloned.1.call-update
  11.3 0.0 reduce-scatter.2.cloned.1.call-start
  11.4 0.0 copy-done
  11.4 0.5 collective-permute-start
  11.9 21.6 %collective-permute-done = bf16[1920,448]{0,1:T(8,128)(2,1)S(1)} collective-permute-done((bf16[1920,448]{0,1:T(8,128)(2,1)S(1)}, bf16[1920,448]{0,1:T(8,128)(2,1)S(1)}, u32[]{:S(2)}, u32[]{:S(2)}) %collective-permute-start) | collective-permute-done | bytes 1720352 | tf_op jit(solution)/shard_map/ppermute | solution.py:24
  33.5 0.0 collective-permute-start.1
  33.5 21.5 %collective-permute-done.1 = bf16[1920,448]{0,1:T(8,128)(2,1)} collective-permute-done((bf16[1920,448]{0,1:T(8,128)(2,1)S(1)}, bf16[1920,448]{0,1:T(8,128)(2,1)}, u32[]{:S(2)}, u32[]{:S(2)}) %collective-permute-start.1) | collective-permute-done | bytes 1720352 | tf_op jit(solution)/shard_map/ppermute | solution.py:24
  55.1 0.0 collective-permute-start.2
  55.1 43.8 %collective-permute-done.2 = bf16[1920,448]{0,1:T(8,128)(2,1)} collective-permute-done((bf16[1920,448]{0,1:T(8,128)(2,1)}, bf16[1920,448]{0,1:T(8,128)(2,1)}, u32[]{:S(2)}, u32[]{:S(2)}) %collective-permute-start.2) | collective-permute-done | bytes 1720352 | tf_op jit(solution)/shard_map/ppermute | solution.py:24
  98.9 2.8 %constant_dynamic-update-slice_fusion.7 = bf16[1920,3584]{0,1:T(8,128)(2,1)} fusion(bf16[1920,448]{0,1:T(8,128)(2,1)} %collective-permute-done.2), kind=kLoop, calls=%fused_computation.71 | loop fusion | bytes 3440640
  101.7 2.8 %constant_dynamic-update-slice_fusion.6 = bf16[1920,3584]{0,1:T(8,128)(2,1)} fusion(bf16[1920,3584]{0,1:T(8,128)(2,1)} %constant_dynamic-update-slice_fusion.7, bf16[1920,448]{0,1:T(8,128)(2,1)} %collective-permute-done.1), kind=kLoop, calls=%fused_computation.70 | loop fusion | bytes 3440640
  104.4 1.3 constant_dynamic-update-slice_fusion.5
  105.8 1.4 constant_dynamic-update-slice_fusion.4
  107.2 2.8 %constant_dynamic-update-slice_fusion.3 = bf16[1920,3584]{0,1:T(8,128)(2,1)} fusion(bf16[1920,3584]{0,1:T(8,128)(2,1)} %constant_dynamic-update-slice_fusion.4, bf16[1920,448]{0,1:T(8,128)(2,1)} %collective-permute-done.2), kind=kLoop, calls=%fused_computation.67 | loop fusion | bytes 3440640
  110.0 2.8 %constant_dynamic-update-slice_fusion.2 = bf16[1920,3584]{0,1:T(8,128)(2,1)} fusion(bf16[1920,3584]{0,1:T(8,128)(2,1)} %constant_dynamic-update-slice_fusion.3, bf16[1920,448]{0,1:T(8,128)(2,1)} %collective-permute-done.1), kind=kLoop, calls=%fused_computation.66 | loop fusion | bytes 3440640
  112.8 1.3 constant_dynamic-update-slice_fusion.1
  114.2 0.0 copy-start.3
  114.2 1.4 constant_dynamic-update-slice_fusion
  115.6 0.0 copy-start.1
  115.6 0.0 copy-start.2
  115.6 0.0 all-gather.3.cloned.1.call-done
  115.6 0.0 all-gather.5.cloned.1.call-done
  115.6 0.0 copy-done.3
  115.6 16.0 %fusion = f32[320,1792]{1,0:T(8,128)} fusion(bf16[1920,3584]{0,1:T(8,128)(2,1)} %constant_dynamic-update-slice_fusion, s32[]{:T(128)S(6)} %select_n.14, bf16[320,1792]{1,0:T(8,128)(2,1)} %all-gather.3.cloned.1.call-done, bf16[1792,1920]{1,0:T(8,128)(2,1)} %all-gather.5.cloned.1.call-done, f32[1920]{0:T(1024)S(1)} %copy-done.3), kind=kOutput, calls=%fused_computation | convolution fusion | flops 4444569600 | bytes 17210884 | tf_op jit(solution)/shard_map/dot_general | solution.py:34
  131.6 0.0 reduce-scatter.2.cloned.1.call-update
  131.7 75.9 %reduce-scatter.2.cloned.1.call-done = f32[40,1792]{1,0:T(8,128)} async-done(((f32[320,1792]{1,0:T(8,128)}), f32[40,1792]{1,0:T(8,128)}) %reduce-scatter.2.cloned.1.call-update) | async-done | bytes 286736 | tf_op jit(solution)/shard_map/reduce_scatter | solution.py:33
  207.5 0.0 copy-done.1
  207.5 0.0 copy-done.2
  207.5 1.7 fusion.51
  (2 shorter events, 0.0 us)
Async XLA Ops:
  6.5 4.9 %copy-start = (bf16[1920,448]{0,1:T(8,128)(2,1)S(1)}, bf16[1920,448]{0,1:T(8,128)(2,1)}, u32[]{:S(2)}) copy-start(bf16[1920,448]{0,1:T(8,128)(2,1)} %param.12) | copy-start | bytes 5160964
  6.5 109.0 %all-gather.3.cloned.1.call-start = ((), (), s32[]{:S(2)}) async-start(), calls=%async_computation.1 | async-start | bytes 1290240 | tf_op jit(solution)/shard_map/all_gather | solution.py:16
  10.6 105.0 %all-gather.5.cloned.1.call-start = ((), (), s32[]{:S(2)}) async-start(), calls=%async_computation.2 | async-start | bytes 8601600 | tf_op jit(solution)/shard_map/all_gather | solution.py:15
  11.3 196.2 %reduce-scatter.2.cloned.1.call-start = ((), (), s32[]{:S(2)}) async-start(), calls=%async_computation.3 | async-start | bytes 2580480 | tf_op jit(solution)/shard_map/reduce_scatter | solution.py:33
  11.4 22.1 %collective-permute-start = (bf16[1920,448]{0,1:T(8,128)(2,1)S(1)}, bf16[1920,448]{0,1:T(8,128)(2,1)S(1)}, u32[]{:S(2)}, u32[]{:S(2)}) collective-permute-start(bf16[1920,448]{0,1:T(8,128)(2,1)S(1)} %copy-done), channel_id=1, source_target_pairs={{0,8},{8,16},{16,24},{24,0},{1,9},{9,17},{17,25},{25,1},{2,10},{10... | collective-permute-start | bytes 5160968 | tf_op jit(solution)/shard_map/ppermute | solution.py:24
  33.5 21.5 %collective-permute-start.1 = (bf16[1920,448]{0,1:T(8,128)(2,1)S(1)}, bf16[1920,448]{0,1:T(8,128)(2,1)}, u32[]{:S(2)}, u32[]{:S(2)}) collective-permute-start(bf16[1920,448]{0,1:T(8,128)(2,1)S(1)} %collective-permute-done), channel_id=1, source_target_pairs={{0,8},{8,16},{16,24},{24,0},{1,9},{9,17},{17,25},{25,1},{2,10},{10... | collective-permute-start | bytes 5160968 | tf_op jit(solution)/shard_map/ppermute | solution.py:24
  55.1 43.8 %collective-permute-start.2 = (bf16[1920,448]{0,1:T(8,128)(2,1)}, bf16[1920,448]{0,1:T(8,128)(2,1)}, u32[]{:S(2)}, u32[]{:S(2)}) collective-permute-start(bf16[1920,448]{0,1:T(8,128)(2,1)} %collective-permute-done.1), channel_id=1, source_target_pairs={{0,8},{8,16},{16,24},{24,0},{1,9},{9,17},{17,25},{25,1},{2,10},{10... | collective-permute-start | bytes 5160968 | tf_op jit(solution)/shard_map/ppermute | solution.py:24
  114.2 1.4 copy-start.3
  115.6 92.0 %copy-start.1 = (bf16[40,1792]{1,0:T(8,128)(2,1)S(1)}, bf16[40,1792]{1,0:T(8,128)(2,1)}, u32[]{:S(2)}) copy-start(bf16[40,1792]{1,0:T(8,128)(2,1)} %param.7) | copy-start | bytes 430084
  115.6 92.0 %copy-start.2 = (f32[1792]{0:T(1024)S(1)}, f32[1792]{0:T(1024)}, u32[]{:S(2)}) copy-start(f32[1792]{0:T(1024)} %param.13) | copy-start | bytes 21508
Sparse Core Ops, SparseCore 0:
  10.7 43.6 all-gather.2
  56.0 59.2 all-gather.4
  131.8 75.7 reduce-scatter.1
